TPU v7x, 256 devices: a whole 4x4x8 slice. The times are simulated.
256 devices in a mesh: rep: 4 (over z_hi), tok: 4 (over z_lo, core), voc: 16 (over x, y).
Axes of the slice: x: 4, y: 4, z: 8 (z_hi: 4, z_lo: 2; z = z_hi * 2 + z_lo), core: 2. Of those that a mesh axis runs over, the one named last changes fastest.
Arguments:
- hidden: bfloat16 [4, 512, 4096], P('rep', ('tok', 'voc')), may hold values from -500 to 500
- targets: int32 [4, 512], P('rep', ('tok', 'voc')), may hold values from 0 to 65535
- unembed: bfloat16 [4, 65536, 4096], P('rep', ('tok', 'voc')), may hold values from -1 to 1
- outer_weight: float32 [8192, 4096], P(('tok', 'voc'), 'rep'), may hold values from -0.9 to 0.9
- momentum: float32 [8192, 4096], P(('tok', 'voc'), 'rep'), may hold values from -0.18 to 0.18
Outputs:
- token_loss: float32 [4, 512], P('rep', ('tok', 'voc'))
- hidden_grad: float32 [4, 512, 4096], P('rep', ('tok', 'voc'))
- new_outer: float32 [8192, 4096], P(('tok', 'voc'), 'rep')
- new_momentum: float32 [8192, 4096], P(('tok', 'voc'), 'rep')
- next_inner: bfloat16 [8192, 4096], P(('tok', 'voc'))
All inputs are finite; a program needn't handle non-finite values.
Results may differ from a plain program's by a relative error of at most 0.0085.
Values may be sent and summed in bfloat16 or wider, within the bound.
No kernel may reach another device: no remote copies, remote signals or barrier semaphores. Data moves between devices by JAX's collectives and lax.ppermute only.
A program may use at most 64 MiB of HBM per device.

v0:
```python
import jax
import jax.numpy as jnp
from jax import lax
from jax.sharding import Mesh
from jax.sharding import PartitionSpec as P

TOK = ("tok_0", "tok_1")
VOC = ("voc_0", "voc_1")
TOK_VOC = ("tok_0", "tok_1", "voc_0", "voc_1")
inner_rate = 0.5
outer_rate = 0.7
momentum_coef = 0.9


def laid_out(pieces, dim):
    dims = list(pieces.shape[1:])
    dims[dim] *= pieces.shape[0]
    return jnp.moveaxis(pieces, 0, dim).reshape(dims)


def stacked_from(value, axes, turns):
    pieces = value[None]
    for k in turns:
        pieces = lax.all_gather(pieces, axes[k], axis=0, tiled=True)
    carried = [lax.axis_size(axes[k]) for k in reversed(turns)]
    pieces = pieces.reshape(*carried, *value.shape)
    turned = sorted(range(len(turns)), key=lambda place: turns[len(turns) - 1 - place])
    return pieces.transpose(*turned, *range(len(turns), pieces.ndim)).reshape(-1, *value.shape)


def gathered_by_axis(value, axes, turns, dim):
    return laid_out(stacked_from(value, axes, turns), dim)


def sent_to_all(value, axis):
    devices = lax.axis_size(axis)
    return lax.all_to_all(
        jnp.broadcast_to(value[None], (devices, *value.shape)), axis, 0, 0, tiled=True
    )


def collected_together(value, axis):
    leaves = jax.tree.leaves(value)
    turns = sorted(range(len(leaves)), key=lambda k: -leaves[k].size)
    width = (1, *leaves[turns[0]].shape)[-1]
    lines = [
        jnp.pad(leaves[k].reshape(-1), (0, -leaves[k].size % width)).reshape(-1, width)
        for k in turns
    ]
    both, at, found = (sent_to_all(jnp.concatenate(lines), axis), 0, {})
    for k, line in zip(turns, lines):
        piece = both[:, at : at + len(line)].reshape(len(both), -1)
        found[k] = piece[:, : leaves[k].size].reshape(-1, *leaves[k].shape)
        at += len(line)
    numbers = iter(range(len(leaves)))
    return jax.tree.map(lambda _: found[next(numbers)], value)


def combined_pairwise(pieces, combine):
    while len(jax.tree.leaves(pieces)[0]) > 1:
        pieces = jax.vmap(combine)(
            *(jax.tree.map(lambda part: part[side::2], pieces) for side in (0, 1))
        )
    return jax.tree.map(lambda part: part[0], pieces)


def combined_all(value, axis, combine):
    pieces = collected_together(value, axis)
    return combined_pairwise(pieces, combine)


def split_up(value, dim, devices):
    dims = value.shape
    pieces = value.reshape(*dims[:dim], devices, dims[dim] // devices, *dims[dim + 1 :])
    return jnp.moveaxis(pieces, dim, 0)


def sum_at_owner(value, axis, dim):
    devices = lax.axis_size(axis)
    pieces = lax.all_to_all(split_up(value, dim, devices), axis, 0, 0, tiled=True)
    return jnp.sum(pieces.astype(jnp.float32), axis=0)


def sent_and_summed(value, axis, dim):
    pieces = split_up(value, dim, lax.axis_size(axis))
    arrived = lax.all_to_all(pieces, axis, split_axis=0, concat_axis=0, tiled=True)
    return arrived.sum(axis=0)


def gather_directly(value, axis, dim):
    pieces = sent_to_all(value, axis)
    return laid_out(pieces, dim)


def combine_stats(earlier, latter):
    row_top = jnp.maximum(earlier[0], latter[0])
    row_total = earlier[1] * jnp.exp(earlier[0] - row_top) + latter[1] * jnp.exp(
        latter[0] - row_top
    )
    return (row_top, row_total, earlier[2] + latter[2])


def nesterov(outer_part, momentum_part, mean_final):
    pseudo_grad = outer_part - mean_final
    moved_momentum = momentum_coef * momentum_part + pseudo_grad
    moved_outer = outer_part - outer_rate * (pseudo_grad + momentum_coef * moved_momentum)
    return (moved_outer, moved_momentum)


def per_device(hidden, targets, unembed, outer_weight, momentum):
    weights = unembed[0]
    vocab_rows, model_width = weights.shape
    tok_rows = hidden.shape[1]
    slab_rows = outer_weight.shape[0]
    logit_scale = model_width ** (-0.5)
    group_index = lax.axis_index(TOK) * lax.axis_size(VOC) + lax.axis_index(VOC)
    every_hidden, every_target = (
        gathered_by_axis(hidden[0], TOK_VOC, (0, 2, 3, 1), 0),
        gathered_by_axis(targets[0], TOK_VOC, (0, 2, 3, 1), 0),
    )
    logits = (
        jnp.einsum("td,vd->tv", every_hidden, weights, preferred_element_type=jnp.float32)
        * logit_scale
    )
    columns = group_index * vocab_rows + lax.broadcasted_iota(jnp.int32, (1, vocab_rows), 1)
    onehot = every_target[:, None] == columns
    target_part = jnp.sum(jnp.where(onehot, logits, 0.0), axis=1)
    local_top = jnp.max(logits, axis=1)
    local_total = jnp.sum(jnp.exp(logits - local_top[:, None]), axis=1)
    row_top, row_total, target_logit = combined_all(
        (local_top, local_total, target_part), TOK_VOC, combine_stats
    )
    log_total = row_top + jnp.log(row_total)
    every_loss = log_total - target_logit
    token_loss = lax.dynamic_slice_in_dim(every_loss, group_index * tok_rows, tok_rows)[None]
    errors = (jnp.exp(logits - log_total[:, None]) - onehot.astype(jnp.float32)).astype(
        jnp.bfloat16
    )
    partial_grad = jnp.dot(errors, weights, preferred_element_type=jnp.float32) * logit_scale
    tok_count = lax.axis_size(TOK)
    split_partial = partial_grad.reshape(tok_count, partial_grad.shape[0] // tok_count, model_width)
    first_section = lax.psum_scatter(
        split_partial.astype(jnp.bfloat16), TOK, scatter_dimension=0, tiled=True
    ).astype(jnp.float32)
    token_grad = sum_at_owner(first_section[0].astype(jnp.bfloat16), VOC, 0)
    slab_errors = errors[:, :slab_rows]
    slab_grad = (
        jnp.einsum("tv,td->vd", slab_errors, every_hidden, preferred_element_type=jnp.float32)
        * logit_scale
    )
    final_slab = weights[:slab_rows].astype(jnp.float32) - inner_rate * slab_grad
    replicas = lax.axis_size("rep")
    mean_final = sent_and_summed(final_slab, "rep", 1) / replicas
    new_outer, new_momentum = nesterov(outer_weight, momentum, mean_final)
    next_inner = gather_directly(new_outer.astype(jnp.bfloat16), "rep", 1)
    return (token_loss, token_grad[None], new_outer, new_momentum, next_inner)


def solution(mesh):
    finer = Mesh(
        mesh.devices.reshape(mesh.shape["rep"], 2, 2, 4, 4),
        ("rep", "tok_0", "tok_1", "voc_0", "voc_1"),
    )
    in_specs = (
        P("rep", TOK_VOC, None),
        P("rep", TOK_VOC),
        P("rep", TOK_VOC, None),
        P(TOK_VOC, "rep"),
        P(TOK_VOC, "rep"),
    )
    out_specs = (
        P("rep", TOK_VOC),
        P("rep", TOK_VOC, None),
        P(TOK_VOC, "rep"),
        P(TOK_VOC, "rep"),
        P(TOK_VOC, None),
    )
    return jax.shard_map(
        per_device, mesh=finer, in_specs=in_specs, out_specs=out_specs, check_vma=False
    )
```

profile of v0, /device:TPU:32, one launch (start us, length us, event | category | flops | bytes accessed | tf_op | source)
XLA Modules:
  0.0 273.8 jit_solution(8645749955817782330)
XLA Ops:
  7.2 0.0 copy-start.3
  7.2 0.0 all-gather.6.cloned.1.call-start
  7.2 5.1 %all_gather.24 = bf16[2,8,4096]{2,1,0:T(8,128)(2,1)S(1)} all-gather(bf16[1,8,4096]{2,1,0:T(8,128)(2,1)} %param.5), channel_id=1, replica_groups=mesh['rep'=4,'tok_0'=2,'tok_1'=2,'voc_0'=4,'voc_1'=4] {'tok_0'}, dimensions={0}, use_global_device_ids=true | all-gather | bytes 196608 | tf_op jit(solution)/shard_map/all_gather | solution.py:24
  12.4 14.2 %all_gather.25 = bf16[8,8,4096]{2,1,0:T(8,128)(2,1)} all-gather(bf16[2,8,4096]{2,1,0:T(8,128)(2,1)S(1)} %all_gather.24), channel_id=1, replica_groups=mesh['rep'=4,'tok_0'=2,'tok_1'=2,'voc_0'=4,'voc_1'=4] {'voc_0'}, dimensions={0}, use_global_device_ids=true | all-gather | bytes 655360 | tf_op jit(solution)/shard_map/all_gather | solution.py:24
  26.5 0.0 all-gather.6.cloned.1.call-update
  26.5 0.0 all-gather.8.cloned.1.call-start
  26.6 35.6 %all-gather.6.cloned.1.call-done = bf16[32,8,4096]{2,1,0:T(8,128)(2,1)} async-done(((bf16[8,8,4096]{2,1,0:T(8,128)(2,1)}), bf16[32,8,4096]{2,1,0:T(8,128)(2,1)}) %all-gather.6.cloned.1.call-update) | async-done | bytes 2097168 | tf_op jit(solution)/shard_map/all_gather | solution.py:24
  62.2 0.0 all-gather.8.cloned.1.call-update
  62.2 0.0 reduce-scatter.2.cloned.1.call-start
  62.2 0.0 copy-done.3
  62.2 4.2 %all-gather = s32[2,1,8]{2,1,0:T(1,128)S(1)} all-gather(s32[1,1,8]{2,1,0:T(1,128)S(1)} %bitcast.74), channel_id=1, replica_groups=mesh['rep'=4,'tok_0'=2,'tok_1'=2,'voc_0'=4,'voc_1'=4] {'tok_0'}, dimensions={0}, use_global_device_ids=true | all-gather | bytes 96 | tf_op jit(solution)/shard_map/all_gather | solution.py:24
  66.5 9.7 %all-gather.1 = s32[4,2,8]{2,1,0:T(2,128)S(1)} all-gather(s32[1,2,8]{2,1,0:T(2,128)S(1)} %bitcast.73), channel_id=1, replica_groups=mesh['rep'=4,'tok_0'=2,'tok_1'=2,'voc_0'=4,'voc_1'=4] {'voc_0'}, dimensions={0}, use_global_device_ids=true | all-gather | bytes 320 | tf_op jit(solution)/shard_map/all_gather | solution.py:24
  76.1 12.0 %all_gather.30 = s32[32,8]{1,0:T(8,128)S(1)} all-gather(s32[8,8]{1,0:T(8,128)S(1)} %bitcast.68), channel_id=1, replica_groups=mesh['rep'=4,'tok_0'=2,'tok_1'=2,'voc_0'=4,'voc_1'=4] {'voc_1'}, dimensions={0}, use_global_device_ids=true | all-gather | bytes 1280 | tf_op jit(solution)/shard_map/all_gather | solution.py:24
  88.1 0.1 copy.22
  88.2 1.8 all-gather.2
  90.0 0.1 copy.23
  90.1 0.1 eq.15
  90.2 0.0 all-gather.8.cloned.1.call-done
  90.3 0.0 copy-start.2
  90.3 2.8 %copy.21 = bf16[2,2,4,4,8,4096]{5,4,3,2,1,0:T(8,128)(2,1)S(1)} copy(bf16[2,2,4,4,8,4096]{5,4,0,2,3,1:T(8,128)(2,1)} %bitcast.57) | data formatting | bytes 8388608 | tf_op jit(solution)/shard_map/transpose | solution.py:28
  93.1 0.0 copy-start
  93.1 3.3 %copy-done.2 = bf16[1,1024,4096]{2,1,0:T(8,128)(2,1)S(1)} copy-done((bf16[1,1024,4096]{2,1,0:T(8,128)(2,1)S(1)}, bf16[1,1024,4096]{2,1,0:T(8,128)(2,1)}, u32[]{:S(2)}) %copy-start.2) | copy-done | bytes 8388632
  96.4 4.6 %multiply_reduce_fusion = (f32[512]{0:T(512)S(1)}, f32[512,1024]{1,0:T(8,128)S(1)}) fusion(bf16[512,4096]{1,0:T(8,128)(2,1)S(1)} %bitcast.53, bf16[1,1024,4096]{2,1,0:T(8,128)(2,1)S(1)} %copy-done.2), kind=kOutput, calls=%fused_computation.15 | convolution fusion | flops 4296015360 | bytes 14682112 | tf_op jit(solution)/shard_map/td,vd->tv/dot_general | solution.py:122
  101.1 0.0 copy-done
  101.1 0.9 exponential_reduce_fusion
  102.0 0.1 broadcast_in_dim.13
  102.1 16.1 %all_to_all.20 = f32[64,3,512]{2,1,0:T(4,128)S(1)} all-to-all(f32[64,3,512]{2,1,0:T(4,128)S(1)} %broadcast_in_dim.13), channel_id=1, replica_groups=mesh['rep'=4,'tok_0'=2,'tok_1'=2,'voc_0'=4,'voc_1'=4] {'tok_0','tok_1','..., dimensions={0} | all-to-all | bytes 786432 | tf_op jit(solution)/shard_map/all_to_all | solution.py:37
  118.2 0.3 fusion.14
  119.1 0.6 fusion.9
  119.7 9.4 %multiply_convert_fusion = bf16[512,4096]{1,0:T(8,128)(2,1)} fusion(bf16[512,1024]{1,0:T(8,128)(2,1)S(1)} %fusion.9, bf16[1,1024,4096]{2,1,0:T(8,128)(2,1)} %param.7), kind=kOutput, calls=%fused_computation.4 | convolution fusion | flops 4299161600 | bytes 13631488 | tf_op jit(solution)/shard_map/dot_general | solution.py:139
  129.1 0.0 reduce-scatter.2.cloned.1.call-update
  129.2 3.3 %fusion.6 = f32[128,4096]{1,0:T(8,128)S(1)} fusion(bf16[512,4096]{1,0:T(8,128)(2,1)} %bitcast.54, bf16[1,1024,4096]{2,1,0:T(8,128)(2,1)} %param.7, bf16[512,1024]{1,0:T(8,128)(2,1)S(1)} %fusion.9), kind=kOutput, calls=%fused_computation.6 | convolution fusion | flops 538443776 | bytes 7471104 | tf_op jit(solution)/shard_map/tv,td->vd/dot_general | solution.py:148
  132.4 0.2 copy.37
  132.7 79.2 %all_to_all.21 = f32[4,128,1024]{2,1,0:T(8,128)S(1)} all-to-all(f32[4,128,1024]{2,1,0:T(8,128)S(1)} %bitcast.55), channel_id=1, replica_groups=mesh['rep'=4,'tok_0'=2,'tok_1'=2,'voc_0'=4,'voc_1'=4] {'rep'}, dimensions={0} | all-to-all | bytes 4194304 | tf_op jit(solution)/shard_map/all_to_all | solution.py:86
  211.9 0.0 copy-start.1
  211.9 0.2 reduce_sum.39
  212.1 0.8 copy-done.1
  212.9 2.2 fusion.13
  215.1 0.1 broadcast_in_dim.28
  215.3 30.5 %all_to_all.22 = bf16[4,128,1024]{2,1,0:T(8,128)(2,1)S(1)} all-to-all(bf16[4,128,1024]{2,1,0:T(8,128)(2,1)S(1)} %broadcast_in_dim.28), channel_id=1, replica_groups=mesh['rep'=4,'tok_0'=2,'tok_1'=2,'voc_0'=4,'voc_1'=4] {'rep'}, dimensions={0} | all-to-all | bytes 2097152 | tf_op jit(solution)/shard_map/all_to_all | solution.py:37
  245.7 0.0 reduce-scatter.2.cloned.1.call-done
  245.7 3.7 %all-to-all-start.1 = ((bf16[16,8,4096]{2,1,0:T(8,128)(2,1)}), bf16[16,8,4096]{2,1,0:T(8,128)(2,1)S(1)}, u32[]{:S(2)}, u32[]{:S(2)}) async-start(bf16[16,8,4096]{2,1,0:T(8,128)(2,1)} %bitcast.60), calls=%async_computation.2 | async-start | bytes 2097152 | tf_op jit(solution)/shard_map/all_to_all | solution.py:80
  249.7 0.6 dynamic-slice_bitcast_fusion
  250.3 0.7 copy.27
  251.0 1.3 copy.28
  252.3 14.2 %all-to-all-done.1 = bf16[16,8,4096]{2,1,0:T(8,128)(2,1)S(1)} async-done(((bf16[16,8,4096]{2,1,0:T(8,128)(2,1)}), bf16[16,8,4096]{2,1,0:T(8,128)(2,1)S(1)}, u32[]{:S(2)}, u32[]{:S(2)}) %all-to-all-start.1) | async-done | bytes 1048608 | tf_op jit(solution)/shard_map/all_to_all | solution.py:80
  266.5 0.8 convert_reduce_fusion
  (48 shorter events, 0.9 us)
Async XLA Ops:
  7.2 55.1 %copy-start.3 = (s32[1,8]{1,0:T(1,128)S(1)}, s32[1,8]{1,0:T(1,128)}, u32[]{:S(2)}) copy-start(s32[1,8]{1,0:T(1,128)} %param.6) | copy-start | bytes 100
  7.2 55.0 %all-gather.6.cloned.1.call-start = ((), (), s32[]{:S(2)}) async-start(), calls=%async_computation.5 | async-start | bytes 2621440 | tf_op jit(solution)/shard_map/all_gather | solution.py:24
  26.5 63.7 %all-gather.8.cloned.1.call-start = ((), (), s32[]{:S(2)}) async-start(), calls=%async_computation.6 | async-start | bytes 6291456 | tf_op jit(solution)/shard_map/all_gather | solution.py:24
  62.2 183.6 %reduce-scatter.2.cloned.1.call-start = ((), (), s32[]{:S(2)}) async-start(), calls=%async_computation.7 | async-start | bytes 5242880 | tf_op jit(solution)/shard_map/reduce_scatter | solution.py:142
  90.3 6.2 %copy-start.2 = (bf16[1,1024,4096]{2,1,0:T(8,128)(2,1)S(1)}, bf16[1,1024,4096]{2,1,0:T(8,128)(2,1)}, u32[]{:S(2)}) copy-start(bf16[1,1024,4096]{2,1,0:T(8,128)(2,1)} %param.7) | copy-start | bytes 25165828
  93.1 8.0 %copy-start = (bf16[2,2,4,4,8,4096]{5,4,3,2,1,0:T(8,128)(2,1)}, bf16[2,2,4,4,8,4096]{5,4,3,2,1,0:T(8,128)(2,1)S(1)}, u32[]{:S(2)}) copy-start(bf16[2,2,4,4,8,4096]{5,4,3,2,1,0:T(8,128)(2,1)S(1)} %copy.21) | copy-start | bytes 12582916
  211.9 1.0 copy-start.1
  245.7 20.8 %all-to-all-start.1 = ((bf16[16,8,4096]{2,1,0:T(8,128)(2,1)}), bf16[16,8,4096]{2,1,0:T(8,128)(2,1)S(1)}, u32[]{:S(2)}, u32[]{:S(2)}) async-start(bf16[16,8,4096]{2,1,0:T(8,128)(2,1)} %bitcast.60), calls=%async_computation.2 | async-start | bytes 2097152 | tf_op jit(solution)/shard_map/all_to_all | solution.py:80
Sparse Core Ops, SparseCore 0:
  26.7 35.4 all-gather.5
  63.9 19.0 all-gather.7
  129.3 89.2 reduce-scatter.1
where the time goes:
time: 274 us
  blocking collectives  173 us (63%)
  waiting for transfers between devices  49.9 us (18%)
  matrix products  17.3 us (6%)
  between operations  14 us (5%)
  local copies, waits for them, and re-layouts  11.2 us (4%)
  other arithmetic  4.85 us (2%)
  starting transfers between devices  3.77 us (1%)
    all_to_all x1, blocking collectives, sent_and_summed(): lax.all_to_all(pieces, axis, split_axis=0, concat_axis=0, tiled=True)  79.2 us
    all_gather x6, blocking collectives, stacked_from(): pieces = lax.all_gather(pieces, axes[k], axis=0, tiled=True)  47 us
    all_to_all x2, blocking collectives, sent_to_all(): lax.all_to_all(jnp.broadcast_to(value[None], (devices, *value.shape)), ax...  46.6 us
    all_gather x2, waiting for transfers between devices, stacked_from(): pieces = lax.all_gather(pieces, axes[k], axis=0, tiled=True)  35.6 us
    all_to_all x1, waiting for transfers between devices, sum_at_owner(): lax.all_to_all(split_up(value, dim, devices), axis, 0, 0, tiled=True)  14.2 us
    dot_general x1, matrix products, per_device(): jnp.dot(errors, weights, preferred_element_type=jnp.float32) * logit_scale  9.42 us
    unnamed x11, local copies, waits for them, and re-layouts  5.56 us
  transfers between devices with their start and end apart: 4, of which 2 were waited for; matrix products, arithmetic and copies ran while one was open for 3% of the time, Pallas kernels for 0%

commit v1 on v0

--- a/solution.py
+++ b/solution.py
@@ -21,7 +21,9 @@
 def stacked_from(value, axes, turns):
     pieces = value[None]
     for k in turns:
-        pieces = lax.all_gather(pieces, axes[k], axis=0, tiled=True)
+        pieces = jnp.concatenate(
+            lax.all_to_all(jnp.stack([pieces] * lax.axis_size(axes[k])), axes[k], 0, 0), axis=0
+        )
     carried = [lax.axis_size(axes[k]) for k in reversed(turns)]
     pieces = pieces.reshape(*carried, *value.shape)
     turned = sorted(range(len(turns)), key=lambda place: turns[len(turns) - 1 - place])

time: 274 us -> 278 us (1.015)
  starting transfers between devices: 3.77 us -> 11.8 us
  waiting for transfers between devices: 49.9 us -> 42.6 us
    all_gather x6 -> x0, blocking collectives: 47 us -> none  [stacked_from(): pieces = lax.all_gather(pieces, axes[k], axis=0, tiled=True)]
    all_to_all x0 -> x6, blocking collectives: none -> 44.2 us  [stacked_from(): lax.all_to_all(jnp.stack([pieces] * lax.axis_size(axes[k])), axes[k], 0, 0)]
    all_gather x2 -> x0, waiting for transfers between devices: 35.6 us -> none  [stacked_from(): pieces = lax.all_gather(pieces, axes[k], axis=0, tiled=True)]
    all_to_all x0 -> x2, waiting for transfers between devices: none -> 28.3 us  [stacked_from(): lax.all_to_all(jnp.stack([pieces] * lax.axis_size(axes[k])), axes[k], 0, 0)]
    all_to_all x0 -> x2, starting transfers between devices: none -> 8.07 us  [stacked_from(): lax.all_to_all(jnp.stack([pieces] * lax.axis_size(axes[k])), axes[k], 0, 0)]
  transfers between devices with their start and end apart: 4 -> 4, of which waited for: 2 -> 3; matrix products, arithmetic and copies ran while one was open for 3% -> 4% of each run, Pallas kernels for 0% -> 0%
where the time goes in v1:
time: 278 us; the launch traced here: 277 us
  blocking collectives  172 us (62%)
  waiting for transfers between devices  42.6 us (15%)
  matrix products  17.3 us (6%)
  between operations  14.3 us (5%)
  starting transfers between devices  11.8 us (4%)
  local copies, waits for them, and re-layouts  11.7 us (4%)
  other arithmetic  7.55 us (3%)
    all_to_all x1, blocking collectives, sent_and_summed(): lax.all_to_all(pieces, axis, split_axis=0, concat_axis=0, tiled=True)  80.9 us
    all_to_all x2, blocking collectives, sent_to_all(): lax.all_to_all(jnp.broadcast_to(value[None], (devices, *value.shape)), ax...  46.6 us
    all_to_all x6, blocking collectives, stacked_from(): lax.all_to_all(jnp.stack([pieces] * lax.axis_size(axes[k])), axes[k], 0, 0)  44.2 us
    all_to_all x2, waiting for transfers between devices, stacked_from(): lax.all_to_all(jnp.stack([pieces] * lax.axis_size(axes[k])), axes[k], 0, 0)  28.3 us
    all_to_all x1, waiting for transfers between devices, sum_at_owner(): lax.all_to_all(split_up(value, dim, devices), axis, 0, 0, tiled=True)  14.2 us
    dot_general x1, matrix products, per_device(): jnp.dot(errors, weights, preferred_element_type=jnp.float32) * logit_scale  9.42 us
    all_to_all x2, starting transfers between devices, stacked_from(): lax.all_to_all(jnp.stack([pieces] * lax.axis_size(axes[k])), axes[k], 0, 0)  8.07 us
  transfers between devices with their start and end apart: 4, of which 3 were waited for; matrix products, arithmetic and copies ran while one was open for 4% of the time, Pallas kernels for 0%

profile of v1, /device:TPU:32, one launch (start us, length us, event | category | flops | bytes accessed | tf_op | source)
XLA Modules:
  0.0 276.9 jit_solution(8394974163799944045)
XLA Ops:
  7.2 0.7 pad_add_fusion.1
  7.9 5.9 %all_to_all.60 = s32[2,1,8]{2,1,0:T(1,128)S(1)} all-to-all(s32[2,1,8]{2,1,0:T(1,128)S(1)} %pad_add_fusion.1), channel_id=1, replica_groups=mesh['rep'=4,'tok_0'=2,'tok_1'=2,'voc_0'=4,'voc_1'=4] {'tok_0'}, dimensions={0} | all-to-all | bytes 128 | tf_op jit(solution)/shard_map/all_to_all | solution.py:25
  13.8 8.3 %all_to_all.61 = s32[4,2,8]{2,1,0:T(2,128)S(1)} all-to-all(s32[4,2,8]{2,1,0:T(2,128)S(1)} %stack.29), channel_id=1, replica_groups=mesh['rep'=4,'tok_0'=2,'tok_1'=2,'voc_0'=4,'voc_1'=4] {'voc_0'}, dimensions={0} | all-to-all | bytes 512 | tf_op jit(solution)/shard_map/all_to_all | solution.py:25
  22.1 0.1 copy.38
  22.2 0.6 stack.30
  22.8 4.5 %all-to-all-start.6 = ((s32[4,8,8]{1,2,0:T(8,128)}), s32[4,8,8]{1,2,0:T(8,128)S(1)}, u32[]{:S(2)}, u32[]{:S(2)}) async-start(s32[4,8,8]{1,2,0:T(8,128)} %stack.30), calls=%async_computation.6 | async-start | bytes 32768 | tf_op jit(solution)/shard_map/all_to_all | solution.py:25
  27.3 0.9 pad_maximum_fusion.1
  28.2 4.4 %all-to-all-done.6 = s32[4,8,8]{1,2,0:T(8,128)S(1)} async-done(((s32[4,8,8]{1,2,0:T(8,128)}), s32[4,8,8]{1,2,0:T(8,128)S(1)}, u32[]{:S(2)}, u32[]{:S(2)}) %all-to-all-start.6) | async-done | bytes 1056 | tf_op jit(solution)/shard_map/all_to_all | solution.py:25
  32.6 0.1 stack_reshape.17
  32.7 0.1 reshape.80
  32.8 3.7 %all_to_all.62 = s32[2,1,256]{2,1,0:T(1,128)S(1)} all-to-all(s32[2,1,256]{2,1,0:T(1,128)S(1)} %reshape.80), channel_id=1, replica_groups=mesh['rep'=4,'tok_0'=2,'tok_1'=2,'voc_0'=4,'voc_1'=4] {'tok_1'}, dimensions={0} | all-to-all | bytes 4096 | tf_op jit(solution)/shard_map/all_to_all | solution.py:25
  36.5 7.0 %all_to_all.63 = bf16[2,1,8,4096]{3,2,1,0:T(8,128)(2,1)S(1)} all-to-all(bf16[2,1,8,4096]{3,2,1,0:T(8,128)(2,1)S(1)} %pad_maximum_fusion.1), channel_id=1, replica_groups=mesh['rep'=4,'tok_0'=2,'tok_1'=2,'voc_0'=4,'voc_1'=4] {'tok_0'}, dimensions={0} | all-to-all | bytes 262144 | tf_op jit(solution)/shard_map/all_to_all | solution.py:25
  43.6 11.9 %all_to_all.64 = bf16[4,2,8,4096]{3,2,1,0:T(8,128)(2,1)S(1)} all-to-all(bf16[4,2,8,4096]{3,2,1,0:T(8,128)(2,1)S(1)} %stack.25), channel_id=1, replica_groups=mesh['rep'=4,'tok_0'=2,'tok_1'=2,'voc_0'=4,'voc_1'=4] {'voc_0'}, dimensions={0} | all-to-all | bytes 1048576 | tf_op jit(solution)/shard_map/all_to_all | solution.py:25
  55.5 1.6 stack.26
  57.0 3.6 %all-to-all-start.2 = ((bf16[4,8,8,4096]{3,2,1,0:T(8,128)(2,1)}), bf16[4,8,8,4096]{3,2,1,0:T(8,128)(2,1)S(1)}, u32[]{:S(2)}, u32[]{:S(2)}) async-start(bf16[4,8,8,4096]{3,2,1,0:T(8,128)(2,1)} %stack.26), calls=%async_computation.2 | async-start | bytes 4194304 | tf_op jit(solution)/shard_map/all_to_all | solution.py:25
  60.6 0.0 reduce-scatter.2.cloned.1.call-start
  60.7 0.5 broadcast.22
  61.2 0.7 reduce
  61.9 0.1 reshape.81
  62.0 0.1 copy.40
  62.1 0.1 eq.15
  62.2 23.9 %all-to-all-done.2 = bf16[4,8,8,4096]{3,2,1,0:T(8,128)(2,1)S(1)} async-done(((bf16[4,8,8,4096]{3,2,1,0:T(8,128)(2,1)}), bf16[4,8,8,4096]{3,2,1,0:T(8,128)(2,1)S(1)}, u32[]{:S(2)}, u32[]{:S(2)}) %all-to-all-start.2) | async-done | bytes 2097184 | tf_op jit(solution)/shard_map/all_to_all | solution.py:25
  86.1 0.4 pad_maximum_fusion
  86.4 7.4 %all_to_all.65 = bf16[2,32,8,4096]{3,2,1,0:T(8,128)(2,1)S(1)} all-to-all(bf16[2,32,8,4096]{3,2,1,0:T(8,128)(2,1)S(1)} %pad_maximum_fusion), channel_id=1, replica_groups=mesh['rep'=4,'tok_0'=2,'tok_1'=2,'voc_0'=4,'voc_1'=4] {'tok_1'}, dimensions={0} | all-to-all | bytes 8388608 | tf_op jit(solution)/shard_map/all_to_all | solution.py:25
  93.8 0.5 copy.37
  94.3 3.2 %slice-done.1 = s8[4194304]{0:T(1024)(128)(4,1)S(1)} async-done(((s8[8388608]{0:T(1024)(128)(4,1)}), s8[4194304]{0:T(1024)(128)(4,1)S(1)}, s32[]{:S(2)}) %slice-start.1) | async-done | bytes 4194328
  97.5 4.6 %multiply_reduce_fusion = (f32[512]{0:T(512)S(1)}, f32[512,1024]{1,0:T(8,128)S(1)}) fusion(bf16[512,4096]{1,0:T(8,128)(2,1)S(1)} %bitcast.61, bf16[1,1024,4096]{2,1,0:T(8,128)(2,1)S(1)} %bitcast.75), kind=kOutput, calls=%fused_computation.16 | convolution fusion | flops 4296015360 | bytes 14682112 | tf_op jit(solution)/shard_map/td,vd->tv/dot_general | solution.py:124
  102.2 0.9 exponential_reduce_fusion
  103.1 0.1 broadcast_in_dim.13
  103.2 16.1 %all_to_all.66 = f32[64,3,512]{2,1,0:T(4,128)S(1)} all-to-all(f32[64,3,512]{2,1,0:T(4,128)S(1)} %broadcast_in_dim.13), channel_id=1, replica_groups=mesh['rep'=4,'tok_0'=2,'tok_1'=2,'voc_0'=4,'voc_1'=4] {'tok_0','tok_1','..., dimensions={0} | all-to-all | bytes 786432 | tf_op jit(solution)/shard_map/all_to_all | solution.py:39
  119.3 0.3 fusion.14
  120.2 0.6 fusion.9
  120.8 9.4 %multiply_convert_fusion = bf16[512,4096]{1,0:T(8,128)(2,1)} fusion(bf16[512,1024]{1,0:T(8,128)(2,1)S(1)} %fusion.9, bf16[1,1024,4096]{2,1,0:T(8,128)(2,1)} %param.7), kind=kOutput, calls=%fused_computation.4 | convolution fusion | flops 4299161600 | bytes 13631488 | tf_op jit(solution)/shard_map/dot_general | solution.py:141
  130.2 0.0 reduce-scatter.2.cloned.1.call-update
  130.3 3.3 %fusion.6 = f32[128,4096]{1,0:T(8,128)S(1)} fusion(bf16[512,4096]{1,0:T(8,128)(2,1)} %bitcast.62, bf16[1,1024,4096]{2,1,0:T(8,128)(2,1)} %param.7, bf16[512,1024]{1,0:T(8,128)(2,1)S(1)} %fusion.9), kind=kOutput, calls=%fused_computation.6 | convolution fusion | flops 538443776 | bytes 7471104 | tf_op jit(solution)/shard_map/tv,td->vd/dot_general | solution.py:150
  133.5 0.2 copy.54
  133.8 80.9 %all_to_all.67 = f32[4,128,1024]{2,1,0:T(8,128)S(1)} all-to-all(f32[4,128,1024]{2,1,0:T(8,128)S(1)} %bitcast.65), channel_id=1, replica_groups=mesh['rep'=4,'tok_0'=2,'tok_1'=2,'voc_0'=4,'voc_1'=4] {'rep'}, dimensions={0} | all-to-all | bytes 4194304 | tf_op jit(solution)/shard_map/all_to_all | solution.py:88
  214.7 0.2 reduce_sum.39
  214.9 0.8 copy-done.1
  215.7 2.2 fusion.13
  217.9 0.1 broadcast_in_dim.28
  218.1 30.5 %all_to_all.68 = bf16[4,128,1024]{2,1,0:T(8,128)(2,1)S(1)} all-to-all(bf16[4,128,1024]{2,1,0:T(8,128)(2,1)S(1)} %broadcast_in_dim.28), channel_id=1, replica_groups=mesh['rep'=4,'tok_0'=2,'tok_1'=2,'voc_0'=4,'voc_1'=4] {'rep'}, dimensions={0} | all-to-all | bytes 2097152 | tf_op jit(solution)/shard_map/all_to_all | solution.py:39
  248.5 3.7 %all-to-all-start.9 = ((bf16[16,8,4096]{2,1,0:T(8,128)(2,1)}), bf16[16,8,4096]{2,1,0:T(8,128)(2,1)S(1)}, u32[]{:S(2)}, u32[]{:S(2)}) async-start(bf16[16,8,4096]{2,1,0:T(8,128)(2,1)} %bitcast.70), calls=%async_computation.10 | async-start | bytes 2097152 | tf_op jit(solution)/shard_map/all_to_all | solution.py:82
  252.5 0.6 dynamic-slice_bitcast_fusion
  253.1 0.7 copy.44
  253.8 1.3 copy.45
  255.1 14.2 %all-to-all-done.9 = bf16[16,8,4096]{2,1,0:T(8,128)(2,1)S(1)} async-done(((bf16[16,8,4096]{2,1,0:T(8,128)(2,1)}), bf16[16,8,4096]{2,1,0:T(8,128)(2,1)S(1)}, u32[]{:S(2)}, u32[]{:S(2)}) %all-to-all-start.9) | async-done | bytes 1048608 | tf_op jit(solution)/shard_map/all_to_all | solution.py:82
  269.3 0.8 convert_reduce_fusion
  (60 shorter events, 1.0 us)
Async XLA Ops:
  22.8 9.8 %all-to-all-start.6 = ((s32[4,8,8]{1,2,0:T(8,128)}), s32[4,8,8]{1,2,0:T(8,128)S(1)}, u32[]{:S(2)}, u32[]{:S(2)}) async-start(s32[4,8,8]{1,2,0:T(8,128)} %stack.30), calls=%async_computation.6 | async-start | bytes 32768 | tf_op jit(solution)/shard_map/all_to_all | solution.py:25
  57.0 29.0 %all-to-all-start.2 = ((bf16[4,8,8,4096]{3,2,1,0:T(8,128)(2,1)}), bf16[4,8,8,4096]{3,2,1,0:T(8,128)(2,1)S(1)}, u32[]{:S(2)}, u32[]{:S(2)}) async-start(bf16[4,8,8,4096]{3,2,1,0:T(8,128)(2,1)} %stack.26), calls=%async_computation.2 | async-start | bytes 4194304 | tf_op jit(solution)/shard_map/all_to_all | solution.py:25
  60.6 187.9 %reduce-scatter.2.cloned.1.call-start = ((), (), s32[]{:S(2)}) async-start(), calls=%async_computation.13 | async-start | bytes 5242880 | tf_op jit(solution)/shard_map/reduce_scatter | solution.py:144
  86.4 7.9 %slice-start = ((s8[8388608]{0:T(1024)(128)(4,1)}), s8[4194304]{0:T(1024)(128)(4,1)S(1)}, s32[]{:S(2)}) async-start(s8[8388608]{0:T(1024)(128)(4,1)} %bitcast.74), calls=%async_computation.14 | async-start | bytes 8388608
  93.8 3.7 %slice-start.1 = ((s8[8388608]{0:T(1024)(128)(4,1)}), s8[4194304]{0:T(1024)(128)(4,1)S(1)}, s32[]{:S(2)}) async-start(s8[8388608]{0:T(1024)(128)(4,1)} %bitcast.74), calls=%async_computation.15 | async-start | bytes 8388608
  94.3 7.8 %copy-start = (bf16[2,2,4,4,8,4096]{5,4,3,2,1,0:T(8,128)(2,1)}, bf16[2,2,4,4,8,4096]{5,4,3,2,1,0:T(8,128)(2,1)S(1)}, u32[]{:S(2)}) copy-start(bf16[2,2,4,4,8,4096]{5,4,3,2,1,0:T(8,128)(2,1)S(1)} %copy.37) | copy-start | bytes 12582916
  214.7 1.0 copy-start.1
  248.5 20.8 %all-to-all-start.9 = ((bf16[16,8,4096]{2,1,0:T(8,128)(2,1)}), bf16[16,8,4096]{2,1,0:T(8,128)(2,1)S(1)}, u32[]{:S(2)}, u32[]{:S(2)}) async-start(bf16[16,8,4096]{2,1,0:T(8,128)(2,1)} %bitcast.70), calls=%async_computation.10 | async-start | bytes 2097152 | tf_op jit(solution)/shard_map/all_to_all | solution.py:82
Sparse Core Ops, SparseCore 0:
  130.4 90.9 reduce-scatter.1
